TPU v7x, 32 devices: a whole 2x2x4 slice. The times are simulated.
32 devices in a mesh: groups: 2 (over y), tensor: 4 (over z), dp: 2 (over x), seq: 2 (over core).
Axes of the slice: x: 2, y: 2, z: 4, core: 2. Of those that a mesh axis runs over, the one named last changes fastest.
Arguments:
- attn_heads: bfloat16 [256, 8192], P(('groups', 'dp', 'seq'), 'tensor'), parts along dimension 0, may hold values from -6 to 6
- out_weight: bfloat16 [8192, 8192], P(('tensor', 'seq')), may hold values from -0.09375 to 0.09375
- residual: bfloat16 [256, 8192], P(('groups', 'dp', 'seq'), 'tensor'), parts along dimension 0, may hold values from -32 to 32
- norm_gain: bfloat16 [8192], P('tensor'), may hold values from 0.099609375 to 1.8984375
Outputs:
- stream: bfloat16 [256, 8192], P(('groups', 'dp', 'seq'), 'tensor'), parts along dimension 0
- normed: bfloat16 [256, 8192], P(('groups', 'dp', 'seq')), parts along dimension 0
There are 2 independent parts, one for each index of `groups`. A program takes and returns all parts, laid end to end along the dimension named above; an argument that names none is the same for every part. Nothing has to cross between parts.
All inputs are finite; a program needn't handle non-finite values.
Results may differ from a plain program's by a relative error of at most 0.0056.
Values may be sent and summed in bfloat16 or wider, within the bound.
A program may use at most 64 MiB of HBM per device.

v0:
```python
import jax
import jax.numpy as jnp
from jax import lax
from jax.sharding import PartitionSpec as P

D = 8192


def block_term(amount, operand, weight, row_count, halves, tensor_size):
    blocks = amount // row_count
    block_width = weight.shape[1] // tensor_size
    span_blocks = min(tensor_size, (blocks + halves - 1) // halves + 1)
    product = jnp.dot(operand, weight, preferred_element_type=jnp.float32)
    product = product.reshape(halves, row_count, span_blocks, block_width)
    product = product.transpose(2, 0, 1, 3).reshape(span_blocks * halves * row_count, block_width)
    return product


def normalize(read, gain_values, square_sum):
    stream_float = read.astype(jnp.float32)
    mean_square = square_sum[:, None] / D
    scaled = (
        stream_float * lax.rsqrt(mean_square + 1e-05) * gain_values.astype(jnp.float32)[None, :]
    )
    return scaled.astype(jnp.bfloat16)


def squares(read):
    stream_float = read.astype(jnp.float32)
    return jnp.sum(stream_float * stream_float, axis=1)


def on_device(attn_heads, out_weight, residual, norm_gain):
    row_count = attn_heads.shape[0]
    half_width = out_weight.shape[0]
    tensor_size = lax.axis_size("tensor")
    halves = lax.axis_size("seq")
    seq_index = lax.axis_index("seq")
    paired_rows = lax.all_gather(attn_heads, "seq", axis=0, tiled=True)
    operand = lax.dynamic_slice_in_dim(paired_rows, seq_index * half_width, half_width, 1)
    attended = lax.psum_scatter(
        block_term(
            row_count * lax.axis_size(("tensor", "seq")),
            operand,
            out_weight,
            row_count,
            halves,
            tensor_size,
        ),
        ("tensor", "seq"),
        scatter_dimension=0,
        tiled=True,
    )
    read = (residual.astype(jnp.float32) + attended).astype(jnp.bfloat16)
    stream_full, gain_full = (
        lax.all_gather(read, "tensor", axis=1, tiled=True),
        lax.all_gather(norm_gain, "tensor", axis=0, tiled=True),
    )
    normed = normalize(stream_full, gain_full, squares(stream_full))
    return (read, normed)


def solution(mesh):
    in_specs = (
        P(("groups", "dp", "seq"), "tensor"),
        P(("tensor", "seq"), None),
        P(("groups", "dp", "seq"), "tensor"),
        P("tensor"),
    )
    out_specs = (P(("groups", "dp", "seq"), "tensor"), P(("groups", "dp", "seq"), None))
    return jax.shard_map(
        on_device, mesh=mesh, in_specs=in_specs, out_specs=out_specs, check_vma=False
    )
```

profile of v0, /device:TPU:0, one launch (start us, length us, event | category | flops | bytes accessed | tf_op | source)
XLA Modules:
  0.0 87.8 jit_solution(3788425832741213699)
XLA Ops:
  7.2 0.0 reduce-scatter.2.cloned.1.call-start
  7.2 2.3 %all_gather.9 = bf16[64,2048]{1,0:T(8,128)(2,1)S(1)} all-gather(bf16[32,2048]{1,0:T(8,128)(2,1)} %param.4), channel_id=1, replica_groups=mesh['groups'=2,'tensor'=4,'dp'=2,'seq'=2] {'seq'}, dimensions={0}, use_global_device_ids=true | all-gather | bytes 393216 | tf_op jit(solution)/shard_map/all_gather | solution.py:39
  9.5 0.0 copy-start.2
  9.5 0.0 copy-start.1
  9.6 8.8 %fusion.3 = f32[64,8192]{1,0:T(8,128)S(1)} fusion(bf16[1024,8192]{1,0:T(8,128)(2,1)} %param.5, bf16[64,2048]{1,0:T(8,128)(2,1)S(1)} %all_gather.9, s32[]{:T(128)S(6)} %select_n.3), kind=kOutput, calls=%fused_computation.6 | convolution fusion | flops 1073741824 | bytes 19005444 | tf_op jit(solution)/shard_map/dot_general | solution.py:13
  18.4 2.4 %reshape.19 = f32[2,32,4,2048]{3,2,1,0:T(4,128)} reshape(f32[64,8192]{1,0:T(8,128)S(1)} %fusion.3) | data formatting | bytes 4194304 | tf_op jit(solution)/shard_map/reshape | solution.py:14
  20.8 4.2 %copy.7 = f32[4,2,32,2048]{3,2,1,0:T(8,128)} copy(f32[4,2,32,2048]{3,0,2,1:T(4,128)} %bitcast.4) | data formatting | bytes 4194304 | tf_op jit(solution)/shard_map/transpose | solution.py:15
  25.0 0.0 reduce-scatter.2.cloned.1.call-update
  25.0 0.0 copy-done.2
  25.0 14.8 %all_gather.11 = bf16[8192]{0:T(1024)(128)(2,1)S(1)} all-gather(bf16[2048]{0:T(1024)(128)(2,1)S(1)} %copy-done.2), channel_id=1, replica_groups=mesh['groups'=2,'tensor'=4,'dp'=2,'seq'=2] {'tensor'}, dimensions={0}, use_global_device_ids=true | all-gather | bytes 20480 | tf_op jit(solution)/shard_map/all_gather | solution.py:57
  39.8 24.1 %reduce-scatter.2.cloned.1.call-done = f32[32,2048]{1,0:T(8,128)} async-done(((f32[256,2048]{1,0:T(8,128)}), f32[32,2048]{1,0:T(8,128)}) %reduce-scatter.2.cloned.1.call-update) | async-done | bytes 262160 | tf_op jit(solution)/shard_map/reduce_scatter | solution.py:41
  63.9 0.0 copy-done.1
  63.9 1.0 %add_convert_fusion = bf16[32,2048]{1,0:T(8,128)(2,1)S(1)} fusion(f32[32,2048]{1,0:T(8,128)} %reduce-scatter.2.cloned.1.call-done, bf16[32,2048]{1,0:T(8,128)(2,1)S(1)} %copy-done.1), kind=kLoop, calls=%fused_computation.5 | loop fusion | flops 196608 | bytes 524288 | tf_op jit(solution)/shard_map/convert_element_type | solution.py:54
  64.9 0.0 copy-start
  64.9 14.9 %all_gather.10 = bf16[32,8192]{1,0:T(8,128)(2,1)S(1)} all-gather(bf16[32,2048]{1,0:T(8,128)(2,1)S(1)} %add_convert_fusion), channel_id=1, replica_groups=mesh['groups'=2,'tensor'=4,'dp'=2,'seq'=2] {'tensor'}, dimensions={1}, use_global_device_ids=true | all-gather | bytes 655360 | tf_op jit(solution)/shard_map/all_gather | solution.py:56
  79.7 0.2 fusion
  80.0 1.0 %fusion.2 = bf16[32,8192]{1,0:T(8,128)(2,1)} fusion(bf16[32,8192]{1,0:T(8,128)(2,1)S(1)} %all_gather.10, f32[8192]{0:T(1024)S(1)} %convert_element_type.19, f32[32]{0:T(128)S(1)} %add_rsqrt_fusion), kind=kLoop, calls=%fused_computation.4 | loop fusion | flops 1048576 | bytes 1081472 | tf_op jit(solution)/shard_map/convert_element_type | solution.py:25
  81.0 0.0 copy-done
  (2 shorter events, 0.0 us)
Async XLA Ops:
  7.2 56.7 %reduce-scatter.2.cloned.1.call-start = ((), (), s32[]{:S(2)}) async-start(), calls=%async_computation.1 | async-start | bytes 2359296 | tf_op jit(solution)/shard_map/reduce_scatter | solution.py:41
  9.5 15.4 %copy-start.2 = (bf16[2048]{0:T(1024)(128)(2,1)S(1)}, bf16[2048]{0:T(1024)(128)(2,1)}, u32[]{:S(2)}) copy-start(bf16[2048]{0:T(1024)(128)(2,1)} %param.7) | copy-start | bytes 12292
  9.5 54.3 %copy-start.1 = (bf16[32,2048]{1,0:T(8,128)(2,1)S(1)}, bf16[32,2048]{1,0:T(8,128)(2,1)}, u32[]{:S(2)}) copy-start(bf16[32,2048]{1,0:T(8,128)(2,1)} %param.6) | copy-start | bytes 393220
  64.9 16.1 %copy-start = (bf16[32,2048]{1,0:T(8,128)(2,1)}, bf16[32,2048]{1,0:T(8,128)(2,1)S(1)}, u32[]{:S(2)}) copy-start(bf16[32,2048]{1,0:T(8,128)(2,1)S(1)} %add_convert_fusion) | copy-start | bytes 393220
Sparse Core Ops, SparseCore 0:
  25.1 38.7 reduce-scatter.1
where the time goes:
time: 88 us; the launch traced here: 87.8 us
  blocking collectives  32 us (36%)
  waiting for transfers between devices  24.1 us (27%)
  between operations  14.1 us (16%)
  matrix products  8.82 us (10%)
  local copies, waits for them, and re-layouts  6.6 us (8%)
  other arithmetic  2.21 us (3%)
    reduce_scatter x1, waiting for transfers between devices, on_device(): lax.psum_scatter(block_term(row_count * lax.axis_size(('tensor', 'seq')),...  24.1 us
    all_gather x1, blocking collectives, on_device(): lax.all_gather(read, 'tensor', axis=1, tiled=True)  14.9 us
    all_gather x1, blocking collectives, on_device(): lax.all_gather(norm_gain, 'tensor', axis=0, tiled=True)  14.8 us
    dot_general x1, matrix products, block_term(): product = jnp.dot(operand, weight, preferred_element_type=jnp.float32)  8.82 us
    transpose x1, local copies, waits for them, and re-layouts, block_term(): product.transpose(2, 0, 1, 3)  4.15 us
    reshape x1, local copies, waits for them, and re-layouts, block_term(): product = product.reshape(halves, row_count, span_blocks, block_width)  2.43 us
    all_gather x1, blocking collectives, on_device(): paired_rows = lax.all_gather(attn_heads, 'seq', axis=0, tiled=True)  2.33 us
  transfers between devices with their start and end apart: 1, of which 1 were waited for; matrix products, arithmetic and copies ran while one was open for 0% of the time, Pallas kernels for 0%

commit v1 on v0

v1 whole, which is shorter than its diff:
```python
import functools

import jax
import jax.numpy as jnp
from jax import lax
from jax.experimental import pallas as pl
from jax.experimental.pallas import tpu as pltpu
from jax.sharding import PartitionSpec as P

MESH = pl.DeviceIdType.MESH
EPS = 1e-05
LAG = 3


def kernel(
    tensor_size, chunk, x_hbm, w_hbm, res_hbm, gain_hbm, stream_ref, normed_ref,
    x_keep, x_give, w_buf, res_buf, gains, core_out, core_in, own_part, part_out, part_in,
    full, squares,
    x_sem, w_sem, xs_sem, xr_sem, gs_sem, gr_sem, cs_sem, cr_sem, ps_sem, pr_sem, fs_sem, fr_sem,
):
    size = tensor_size
    pairs = size // 2
    z = lax.axis_index("tensor")
    core = lax.axis_index("seq")
    rows, width = res_hbm.shape
    depth, total = w_hbm.shape
    splits = width // chunk
    pair, parity = z // 2, lax.rem(z, 2)

    def peer(k):
        return {"tensor": lax.rem(z + k, size)}

    other_core = {"seq": 1 - core}

    order = [(s, k) for s in range(splits) for k in list(range(1, size)) + [0]]

    def x_cols(which):
        return pl.ds(pl.multiple_of(which * depth, depth), depth)

    keep = pltpu.make_async_copy(x_hbm.at[:, x_cols(core)], x_keep.at[0], x_sem.at[0])
    give = pltpu.make_async_copy(x_hbm.at[:, x_cols(1 - core)], x_give, x_sem.at[1])
    give.start()
    keep.start()
    loads = []
    for i, (s, k) in enumerate(order):
        start = pl.multiple_of(lax.rem(z + k, size) * width + s * chunk, chunk)
        load = pltpu.make_async_copy(w_hbm.at[:, pl.ds(start, chunk)], w_buf.at[i], w_sem.at[i])
        load.start()
        loads.append(load)
        if i == 1:
            res_load = pltpu.make_async_copy(res_hbm, res_buf, x_sem.at[2])
            gain_load = pltpu.make_async_copy(gain_hbm, gains.at[z], x_sem.at[3])
            res_load.start()
            gain_load.start()

    barrier = pltpu.get_barrier_semaphore()
    pl.semaphore_signal(barrier, inc=1, device_id=other_core, device_id_type=MESH)
    for k in range(1, size):
        pl.semaphore_signal(barrier, inc=1, device_id=peer(k), device_id_type=MESH)
    give.wait()
    pl.semaphore_wait(barrier, size)

    swap = pltpu.make_async_remote_copy(
        x_give, x_keep.at[1], xs_sem, xr_sem, device_id=other_core, device_id_type=MESH
    )
    swap.start()
    sends = [swap]
    gain_load.wait()
    gain_copies = []
    for k in range(1, size):
        copy = pltpu.make_async_remote_copy(
            gains.at[z], gains.at[z], gs_sem.at[k], gr_sem.at[k], device_id=peer(k), device_id_type=MESH
        )
        copy.start()
        gain_copies.append(copy)
    keep.wait()
    swap.wait_recv()
    res_load.wait()

    x = x_keep[...].reshape(2 * rows, depth)
    core_copies = {}
    part_copies = {}
    count = len(order)
    for i in range(count + LAG):
        if i < count:
            loads[i].wait()
            product = jnp.dot(x, w_buf[i], preferred_element_type=jnp.float32)
            core_out[i] = product[rows:]
            own_part[i] = product[:rows]
            copy = pltpu.make_async_remote_copy(
                core_out.at[i], core_in.at[i], cs_sem.at[i], cr_sem.at[i],
                device_id=other_core, device_id_type=MESH,
            )
            copy.start()
            core_copies[i] = copy
        j = i - LAG
        if j >= 0:
            s, k = order[j]
            core_copies[j].wait_recv()
            both = own_part[j] + core_in[j]
            if k == 0:
                own_part[j] = both + res_buf[:, s * chunk:(s + 1) * chunk].astype(jnp.float32)
            else:
                part_out[k, s] = both.astype(jnp.bfloat16)
                copy = pltpu.make_async_remote_copy(
                    part_out.at[k, s], part_in.at[k, s], ps_sem.at[k, s], pr_sem.at[k, s],
                    device_id=peer(k), device_id_type=MESH,
                )
                copy.start()
                part_copies[k, s] = copy

    def note_squares(block, s, value):
        value = value.astype(jnp.float32)
        square = value * value
        squares[block, s] = functools.reduce(
            lambda a, b: a + b, [square[:, c:c + 128] for c in range(0, chunk, 128)]
        )

    gathers = []
    direct = {}
    for s in range(splits):
        at = order.index((s, 0))
        value = own_part[at]
        for k in range(1, size):
            part_copies[k, s].wait_recv()
            value = value + part_in[k, s].astype(jnp.float32)
        value = value.astype(jnp.bfloat16)
        full[z, s] = value
        for m in range(1, pairs):
            target = 2 * lax.rem(pair + m, pairs) + parity
            copy = pltpu.make_async_remote_copy(
                full.at[z, s], full.at[z, s],
                fs_sem.at[0, m, s], fr_sem.at[0, (pairs - m) % pairs, s],
                device_id={"tensor": target}, device_id_type=MESH,
            )
            copy.start()
            direct[(pairs - m) % pairs, s] = copy
        copy = pltpu.make_async_remote_copy(
            full.at[z, s], full.at[z, s], fs_sem.at[1, 0, s], fr_sem.at[1, 0, s],
            device_id={"tensor": 2 * pair + 1 - parity}, device_id_type=MESH,
        )
        copy.start()
        gathers.append((0, s, copy))
        stream_ref[:, s * chunk:(s + 1) * chunk] = value
        note_squares(z, s, value)

    for s in range(splits):
        for m in range(1, pairs):
            direct[m, s].wait_recv()
            block = 2 * lax.rem(pair + m, pairs) + parity
            copy = pltpu.make_async_remote_copy(
                full.at[block, s], full.at[block, s], fs_sem.at[1, m, s], fr_sem.at[1, m, s],
                device_id={"tensor": 2 * pair + 1 - parity}, device_id_type=MESH,
            )
            copy.start()
            gathers.append((m, s, copy))
            note_squares(block, s, full[block, s])
    for m, s, copy in gathers:
        copy.wait_recv()
        block = 2 * lax.rem(pair + m, pairs) + 1 - parity
        note_squares(block, s, full[block, s])

    summed = functools.reduce(
        lambda a, b: a + b, [squares[block, s] for block in range(size) for s in range(splits)]
    )
    scale = lax.rsqrt(jnp.sum(summed, axis=1, keepdims=True) / total + EPS)
    for copy in gain_copies:
        copy.wait_recv()
    for block in range(size):
        gain = gains[block].astype(jnp.float32)
        for s in range(splits):
            first = block * width + s * chunk
            normed_ref[:, first:first + chunk] = (
                full[block, s].astype(jnp.float32) * scale * gain[:, s * chunk:(s + 1) * chunk]
            ).astype(jnp.bfloat16)

    for copy in (
        sends + gain_copies + list(core_copies.values()) + list(part_copies.values())
        + list(direct.values()) + [copy for _, _, copy in gathers]
    ):
        copy.wait_send()


def on_device(attn_heads, out_weight, residual, norm_gain):
    rows, width = residual.shape
    depth, total = out_weight.shape
    size = total // width
    chunk = min(width, 512)
    splits = width // chunk
    count = size * splits
    half, single = jnp.bfloat16, jnp.float32
    any_space = pl.BlockSpec(memory_space=pl.ANY)
    vmem = pl.BlockSpec(memory_space=pltpu.VMEM)
    dma = pltpu.SemaphoreType.DMA
    return pl.pallas_call(
        functools.partial(kernel, size, chunk),
        out_shape=(
            jax.ShapeDtypeStruct((rows, width), half),
            jax.ShapeDtypeStruct((rows, total), half),
        ),
        in_specs=[any_space] * 4,
        out_specs=(vmem, vmem),
        scratch_shapes=[
            pltpu.VMEM((2, rows, depth), half),
            pltpu.VMEM((rows, depth), half),
            pltpu.VMEM((count, depth, chunk), half),
            pltpu.VMEM((rows, width), half),
            pltpu.VMEM((size, 1, width), half),
            pltpu.VMEM((count, rows, chunk), single),
            pltpu.VMEM((count, rows, chunk), single),
            pltpu.VMEM((count, rows, chunk), single),
            pltpu.VMEM((size, splits, rows, chunk), half),
            pltpu.VMEM((size, splits, rows, chunk), half),
            pltpu.VMEM((size, splits, rows, chunk), half),
            pltpu.VMEM((size, splits, rows, 128), single),
            dma((4,)),
            dma((count,)),
            dma,
            dma,
            dma((size,)),
            dma((size,)),
            dma((count,)),
            dma((count,)),
            dma((size, splits)),
            dma((size, splits)),
            dma((2, size // 2, splits)),
            dma((2, size // 2, splits)),
        ],
        compiler_params=pltpu.CompilerParams(
            collective_id=0, has_side_effects=True, vmem_limit_bytes=48 * 1024 * 1024
        ),
    )(attn_heads, out_weight, residual, norm_gain.reshape(1, width))


def solution(mesh):
    rows = P(("groups", "dp", "seq"), "tensor")
    in_specs = (rows, P(("tensor", "seq"), None), rows, P("tensor"))
    out_specs = (rows, P(("groups", "dp", "seq"), None))
    return jax.shard_map(
        on_device, mesh=mesh, in_specs=in_specs, out_specs=out_specs, check_vma=False
    )
```

time: 88 us -> 35.2 us (0.40)
  blocking collectives: 32 us -> 0 us
  Pallas kernels: 0 us -> 30.5 us
  waiting for transfers between devices: 24.1 us -> 0 us
  between operations: 14.1 us -> 0.64 us
  matrix products: 8.82 us -> 0 us
  local copies, waits for them, and re-layouts: 6.6 us -> 3.95 us
  other arithmetic: 2.21 us -> 0 us
    all_gather x3 -> x0, blocking collectives: 32 us -> none  [the longest x1 14.9 us: on_device(): lax.all_gather(read, 'tensor', axis=1, tiled=True)]
    pallas_call x0 -> x1, Pallas kernels: none -> 30.5 us  [on_device(): pl.pallas_call(functools.partial(kernel, size, chunk), out_shape=(jax.Sha...]
    reduce_scatter x1 -> x0, waiting for transfers between devices: 24.1 us -> none  [on_device(): lax.psum_scatter(block_term(row_count * lax.axis_size(('tensor', 'seq')),...]
    dot_general x1 -> x0, matrix products: 8.82 us -> none  [block_term(): product = jnp.dot(operand, weight, preferred_element_type=jnp.float32)]
    transpose x1 -> x0, local copies, waits for them, and re-layouts: 4.15 us -> none  [block_term(): product.transpose(2, 0, 1, 3)]
    unnamed x6, local copies, waits for them, and re-layouts: 0.01 us -> 3.26 us
    convert_element_type x3 -> x0, other arithmetic: 1.97 us -> none  [the longest x1 0.99 us: normalize(): return scaled.astype(jnp.bfloat16)]
    reshape x1, local copies, waits for them, and re-layouts: 2.43 us -> 0.69 us  [on_device(): norm_gain.reshape(1, width)]
  transfers between devices with their start and end apart: 1 -> 0, of which waited for: 1 -> 0; matrix products, arithmetic and copies ran while one was open for 0% -> 0% of each run, Pallas kernels for 0% -> 0%
where the time goes in v1:
time: 35.2 us; the launch traced here: 35.1 us
  Pallas kernels  30.5 us (87%)
  local copies, waits for them, and re-layouts  3.95 us (11%)
  between operations  0.64 us (2%)
    pallas_call x1, Pallas kernels, on_device(): pl.pallas_call(functools.partial(kernel, size, chunk), out_shape=(jax.Sha...  30.5 us
    unnamed x6, local copies, waits for them, and re-layouts  3.26 us

profile of v1, /device:TPU:0, one launch (start us, length us, event | category | flops | bytes accessed | tf_op | source)
XLA Modules:
  0.0 35.1 jit_solution(10794052617216267022)
XLA Ops:
  0.6 0.7 %reshape.7.gain_hbm = bf16[1,2048]{1,0:T(2,128)(2,1)S(1)} reshape(bf16[2048]{0:T(1024)(128)(2,1)} %param.7) | data formatting | bytes 8192 | tf_op jit(solution)/shard_map/reshape | solution.py:232
  1.3 0.0 copy-start
  1.3 0.9 %copy-done = bf16[32,2048]{1,0:T(8,128)(2,1)S(1)} copy-done((bf16[32,2048]{1,0:T(8,128)(2,1)S(1)}, bf16[32,2048]{1,0:T(8,128)(2,1)}, u32[]{:S(2)}) %copy-start) | copy-done | bytes 131096
  2.2 0.0 copy-start.1
  2.2 0.9 %copy-done.1 = bf16[32,2048]{1,0:T(8,128)(2,1)S(1)} copy-done((bf16[32,2048]{1,0:T(8,128)(2,1)S(1)}, bf16[32,2048]{1,0:T(8,128)(2,1)}, u32[]{:S(2)}) %copy-start.1) | copy-done | bytes 131096
  3.1 30.5 %shard_map.59 = (bf16[32,2048]{1,0:T(8,128)(2,1)S(1)}, bf16[32,8192]{1,0:T(8,128)(2,1)S(1)}) custom-call(bf16[32,2048]{1,0:T(8,128)(2,1)S(1)} %copy-done, bf16[1024,8192]{1,0:T(8,128)(2,1)} %w_hbm.1, bf16[32,2048]{1,0:T(8,128)(2,1)S(1)} %copy-done.1, bf16[1,2048]{1,0:T(2,128)(2,1)S(1)} %reshape.7.gain_hbm), custom_call_target="tpu_custom_call" | custom-call | tf_op jit(solution)/shard_map/pallas_call | solution.py:195
  33.6 0.7 %copy.8 = bf16[32,2048]{1,0:T(8,128)(2,1)} copy(bf16[32,2048]{1,0:T(8,128)(2,1)S(1)} %get-tuple-element.4) | data formatting | bytes 262144
  34.3 0.8 %copy.9 = bf16[32,8192]{1,0:T(8,128)(2,1)} copy(bf16[32,8192]{1,0:T(8,128)(2,1)S(1)} %get-tuple-element.5) | data formatting | bytes 1048576
Async XLA Ops:
  1.3 0.9 %copy-start = (bf16[32,2048]{1,0:T(8,128)(2,1)S(1)}, bf16[32,2048]{1,0:T(8,128)(2,1)}, u32[]{:S(2)}) copy-start(bf16[32,2048]{1,0:T(8,128)(2,1)} %x_hbm.1) | copy-start | bytes 393220
  2.2 0.9 %copy-start.1 = (bf16[32,2048]{1,0:T(8,128)(2,1)S(1)}, bf16[32,2048]{1,0:T(8,128)(2,1)}, u32[]{:S(2)}) copy-start(bf16[32,2048]{1,0:T(8,128)(2,1)} %res_hbm.1) | copy-start | bytes 393220
